TPU v7x, 32 devices: a whole 2x2x4 slice. The times are simulated.
32 devices in a mesh: groups: 2 (over y), seq: 4 (over z), head: 4 (over x, core).
Axes of the slice: x: 2, y: 2, z: 4, core: 2. Of those that a mesh axis runs over, the one named last changes fastest.
Arguments:
- queries: bfloat16 [2048, 8192], P(('groups', 'seq'), 'head'), parts along dimension 0, may hold values from -16 to 16
- keys: bfloat16 [2048, 1024], P(('groups', 'seq'), 'head'), parts along dimension 0, may hold values from -16 to 16
- values: bfloat16 [2048, 1024], P(('groups', 'seq'), 'head'), parts along dimension 0, may hold values from -6 to 6
- prompt_len: int32 [2], P('groups'), parts along dimension 0, may hold values from 256 to 1024
- page_dest: int32 [8, 2], P('groups'), parts along dimension 0, may hold values from 0 to 3, all different within a row; in each aligned block of 4 rows (0 to 3, 4 to 7, ...) at most 4 rows name the same one
Outputs:
- attended: bfloat16 [2048, 8192], P(('groups', 'seq'), 'head'), parts along dimension 0
- decode_page_cache: bfloat16 [32, 128, 2048], P(('groups', 'seq'), None, 'head'), parts along dimension 0
There are 2 independent parts, one for each index of `groups`. A program takes and returns all parts, laid end to end along the dimension named above; each array names one. Nothing has to cross between parts.
Inputs may be any that keep to these rules, and one draw needn't show every extreme that they name: `page_dest`: row s names the decode devices of the 2 pages of tokens s * 256 to (s + 1) * 256 - 1, all different within a row; no device is named more than 4 times in all, and some device exactly 4 times.
All inputs are finite; a program needn't handle non-finite values.
Results may differ from a plain program's by a relative error of at most 0.005.
Values may be sent and summed in bfloat16 or wider, within the bound.
A program may use at most 64 MiB of HBM per device.

v0:
```python
import math
import jax
import jax.numpy as jnp
from jax import lax
from jax.sharding import PartitionSpec as P

HEAD_SIZE = 128
PAGE_TOKENS = 128
NEG_FILL = -1e30


def blank_state(kv_heads, group_size, query_count):
    return (
        jnp.full((kv_heads, group_size, query_count), NEG_FILL, jnp.float32),
        jnp.zeros((kv_heads, group_size, query_count), jnp.float32),
        jnp.zeros((kv_heads, group_size, query_count, HEAD_SIZE), jnp.float32),
    )


def attend_block(
    query_state, query_block, query_pos, key_block, value_block, block_start, prompt_end
):
    key_count = key_block.shape[0]
    kv_heads = key_block.shape[1] // HEAD_SIZE
    keys_split = key_block.reshape(key_count, kv_heads, HEAD_SIZE)
    values_split = value_block.reshape(key_count, kv_heads, HEAD_SIZE)
    scores = jnp.einsum(
        "rkgd,pkd->kgrp", query_block, keys_split, preferred_element_type=jnp.float32
    )
    scores = scores * (1.0 / math.sqrt(HEAD_SIZE))
    key_pos = block_start + jnp.arange(key_count, dtype=jnp.int32)
    allowed = (key_pos[None, :] <= query_pos[:, None]) & (key_pos[None, :] < prompt_end)
    scores = jnp.where(allowed, scores, NEG_FILL)
    old_max = query_state[0]
    new_max = jnp.maximum(old_max, jnp.max(scores, axis=-1))
    weights = jnp.where(allowed, jnp.exp(scores - new_max[..., None]), 0.0)
    factor = jnp.exp(old_max - new_max)
    denominator = query_state[1] * factor + jnp.sum(weights, axis=-1)
    accumulated = query_state[2] * factor[..., None] + jnp.einsum(
        "kgrp,pkd->kgrd",
        weights.astype(jnp.bfloat16),
        values_split,
        preferred_element_type=jnp.float32,
    )
    return (new_max, denominator, accumulated)


def finish(query_state, query_pos, prompt_end):
    query_live = query_pos < prompt_end
    safe_total = jnp.where(query_live[None, None, :], query_state[1], 1.0)
    result = jnp.where(query_live[None, None, :, None], query_state[2] / safe_total[..., None], 0.0)
    query_count = query_pos.shape[0]
    return result.transpose(2, 0, 1, 3).reshape(query_count, -1).astype(jnp.bfloat16)


def join_pages(key_rows, value_rows):
    page_count = key_rows.shape[0] // PAGE_TOKENS
    kv_heads = key_rows.shape[1] // HEAD_SIZE
    stacked = jnp.stack(
        (
            key_rows.reshape(page_count, PAGE_TOKENS, kv_heads, HEAD_SIZE),
            value_rows.reshape(page_count, PAGE_TOKENS, kv_heads, HEAD_SIZE),
        ),
        axis=3,
    )
    return stacked.reshape(page_count, PAGE_TOKENS, 2 * key_rows.shape[1])


def slot_pages(page_dest, owner, slots):
    flat_dest = page_dest.reshape(-1)
    page_order = jnp.arange(flat_dest.shape[0], dtype=jnp.int32)
    same_dest = flat_dest[:, None] == flat_dest[None, :]
    dest_rank = jnp.sum(same_dest & (page_order[None, :] < page_order[:, None]), axis=1)
    matched = (flat_dest[:, None] == owner) & (
        dest_rank[:, None] == jnp.arange(slots, dtype=jnp.int32)[None, :]
    )
    page_index = jnp.sum(jnp.where(matched, page_order[:, None], 0), axis=0)
    present = jnp.any(matched, axis=0)
    return (flat_dest, page_index, present)


def place_pages(stored, key_block, value_block, block_start, prompt_end, page_index, present):
    key_pos = block_start + jnp.arange(key_block.shape[0], dtype=jnp.int32)
    token_present = (key_pos < prompt_end)[:, None]
    block_pages = join_pages(
        jnp.where(token_present, key_block, 0), jnp.where(token_present, value_block, 0)
    )
    page_count = block_pages.shape[0]
    local_index = page_index - block_start // PAGE_TOKENS
    inside = present & (local_index >= 0) & (local_index < page_count)
    picked = block_pages[jnp.clip(local_index, 0, page_count - 1)]
    return jnp.where(inside[:, None, None], picked, stored)


def local(queries, keys, values, prompt_len, page_dest):
    shard_rows = queries.shape[0]
    kv_width = keys.shape[1]
    kv_heads = kv_width // HEAD_SIZE
    group_size = queries.shape[1] // kv_width
    seq_index = lax.axis_index("seq")
    prompt_end = prompt_len[0]
    per_device = page_dest.shape[1]
    slots = 2 * per_device
    flat_dest, page_index, present = slot_pages(page_dest, seq_index, slots)
    own_rows = seq_index * shard_rows + jnp.arange(shard_rows, dtype=jnp.int32)
    query_parts = (queries,)
    positions = (own_rows,)
    shaped = tuple(
        (
            part_rows.reshape(part_rows.shape[0], kv_heads, group_size, HEAD_SIZE)
            for part_rows in query_parts
        )
    )
    states = tuple(
        (blank_state(kv_heads, group_size, part_rows.shape[0]) for part_rows in query_parts)
    )
    page_store = jnp.zeros((slots, PAGE_TOKENS, 2 * kv_width), jnp.bfloat16)
    key_piece = lax.all_gather(keys, "seq", axis=0, tiled=True)
    value_piece = lax.all_gather(values, "seq", axis=0, tiled=True)
    block_count = key_piece.shape[0] // shard_rows
    per_step = max(1, min(block_count, 512 // shard_rows))
    while block_count % per_step:
        per_step -= 1
    step_rows = per_step * shard_rows
    steps_count = block_count // per_step
    key_blocks = key_piece.reshape(steps_count, step_rows, kv_width)
    value_blocks = value_piece.reshape(steps_count, step_rows, kv_width)

    def one_block(inner_carry, block_item):
        block_states, stored = inner_carry
        key_block, value_block, number = block_item
        block_start = number * step_rows
        updated = []
        for query_state, query_block, query_pos in zip(block_states, shaped, positions):
            needed = block_start <= jnp.minimum(query_pos[-1], prompt_end - 1)
            updated.append(
                lax.cond(
                    needed,
                    lambda kept: attend_block(
                        kept,
                        query_block,
                        query_pos,
                        key_block,
                        value_block,
                        block_start,
                        prompt_end,
                    ),
                    lambda kept: kept,
                    query_state,
                )
            )
        stored = place_pages(
            stored, key_block, value_block, block_start, prompt_end, page_index, present
        )
        return ((tuple(updated), stored), None)

    result, unused = lax.scan(
        one_block,
        (states, page_store),
        (key_blocks, value_blocks, jnp.arange(steps_count, dtype=jnp.int32)),
    )
    final_states, stored = result
    outputs = [
        finish(query_state, query_pos, prompt_end)
        for query_state, query_pos in zip(final_states, positions)
    ]
    attended = outputs[0]
    return (attended, stored)


def solution(mesh):
    return jax.shard_map(
        local,
        mesh=mesh,
        in_specs=(
            P(("groups", "seq"), "head"),
            P(("groups", "seq"), "head"),
            P(("groups", "seq"), "head"),
            P("groups"),
            P("groups", None),
        ),
        out_specs=(P(("groups", "seq"), "head"), P(("groups", "seq"), None, "head")),
        check_vma=False,
    )
```

profile of v0, /device:TPU:26, one launch (start us, length us, event | category | flops | bytes accessed | tf_op | source)
XLA Modules:
  0.0 76.9 jit_solution(3035175965505265752)
XLA Ops:
  1.3 0.7 slice.5
  2.7 0.8 copy.34
  3.4 0.1 broadcast_in_dim_reshape.2
  3.5 0.2 convert_reduce_fusion
  3.7 0.1 fusion.20
  3.8 0.1 select_reduce_fusion
  4.0 16.3 %all_gather.6 = bf16[1024,256]{1,0:T(8,128)(2,1)} all-gather(bf16[256,256]{1,0:T(8,128)(2,1)} %param.10), channel_id=1, replica_groups=mesh['groups'=2,'seq'=4,'head'=4] {'seq'}, dimensions={0}, use_global_device_ids=true | all-gather | bytes 655360 | tf_op jit(solution)/shard_map/all_gather | solution.py:118
  20.3 16.4 %all_gather.7 = bf16[1024,256]{1,0:T(8,128)(2,1)} all-gather(bf16[256,256]{1,0:T(8,128)(2,1)} %param.11), channel_id=1, replica_groups=mesh['groups'=2,'seq'=4,'head'=4] {'seq'}, dimensions={0}, use_global_device_ids=true | all-gather | bytes 655360 | tf_op jit(solution)/shard_map/all_gather | solution.py:119
  36.7 1.5 %copy.33 = bf16[256,2048]{0,1:T(8,128)(2,1)S(1)} copy(bf16[256,2048]{1,0:T(8,128)(2,1)} %param.9) | data formatting | bytes 2097152 | tf_op args[0]
  38.2 0.7 copy.35
  38.9 1.6 %broadcast_in_dim.106 = f32[2,8,256,128]{3,2,1,0:T(8,128)} broadcast(f32[]{:T(128)} %constant.102.clone.1), dimensions={} | broadcast | bytes 2097156 | tf_op jit(solution)/shard_map/broadcast_in_dim | solution.py:16
  40.4 31.5 %while.20 = (s32[]{:T(128)}, f32[2,8,256]{2,1,0:T(8,128)S(1)}, f32[2,8,256]{2,1,0:T(8,128)S(1)}, f32[2,8,256,128]{3,2,1,0:T(8,128)}, bf16[4,128,512]{1,2,0:T(8,1...) while((s32[]{:T(128)}, f32[2,8,256]{2,1,0:T(8,128)S(1)}, ...), condition=%wide.region_8.9_spmd.clone, body=%wide.region_3.8_spmd.clone.sunk | while | flops 1103377152 | bytes 57424572 | solution.py:157
  40.4 0.7 dynamic_slice.31
  41.9 0.7 add_compare_fusion.2
  42.5 1.1 %constant_dynamic-slice_fusion.3 = (bf16[1,512,256]{2,1,0:T(8,128)(2,1)S(1)}, bf16[1,512,256]{2,1,0:T(8,128)(2,1)S(1)}) fusion(bf16[2,512,256]{2,1,0:T(8,128)(2,1)} %get-tuple-element.556, s32[]{:T(128)S(6)} %copy.67, bf16[2,512,256]{2,1,0:T(8,128)(2,1)} %get-tuple-element.555), kind=kLoop, calls=%fused_computation.31.clone.1 | loop fusion | bytes 1048580 | tf_op jit(solution)/shard_map/while/body/jit(dynamic_index_in_dim)/dynamic_slice | solution.py:157
  43.6 0.1 squeeze.31
  43.7 0.1 squeeze.32
  43.8 1.1 %broadcast_select_fusion.4 = (bf16[4,128,2,1,128]{4,2,1,0,3:T(2,128)(2,1)S(1)}, bf16[4,128,2,1,128]{4,2,1,0,3:T(2,128)(2,1)S(1)}) fusion(bf16[4,128,2,1,128]{4,2,1,0,3:T(2,128)(2,1)S(1)} %squeeze.31, pred[4,128]{1,0:T(4,128)(4,1)S(1)} %add_compare_fusion.2, bf16[4,128,2,1,128]{4,2,1,0,3:T(2,128)(2,1)S(1)} %squeeze.32), kind=kLoop, calls=%fused_computation.25.clone.1 | loop fusion | flops 262144 | bytes 1049088 | tf_op jit(solution)/shard_map/while/body/eval_jaxpr/jit(_where)/select_n | solution.py:86
  44.9 0.7 pad_maximum_fusion.2
  45.6 0.4 copy.55
  46.1 0.6 gather_fusion
  46.7 0.2 select_select_fusion.2
  46.9 9.3 %conditional.3 = ((f32[2,8,256]{2,1,0:T(8,128)S(1)}, f32[2,8,256]{2,1,0:T(8,128)S(1)}, f32[2,8,256,128]{3,2,1,0:T(8,128)})) conditional(s32[]{:T(128)} %convert_element_type.41, (f32[2,8,256]{2,1,0:T(8,128)S(1)}, f32[2,8,256]{2,1,0:T(8,128)S(1)}, f32[2,8,256,128]{3,2,1,0:T(8,128)}) %tuple.62, (s32[]{:T(128)}, s32[]{:T(128)}, s32[]{:T(128)}, ...), branch_computations={%region_4.4_spmd, %region_5.7_spmd} | conditional | flops 1102325504 | bytes 49553512 | solution.py:137
  46.9 0.7 broadcast_compare_fusion
  47.6 0.2 compare_and_fusion
  47.8 0.1 reshape.144
  47.9 0.1 reshape.145
  47.9 0.0 copy-start
  48.0 1.4 %fusion.2 = (f32[2,8,256]{2,1,0:T(8,128)S(1)}, f32[2,512,256,8]{2,1,3,0:T(8,128)S(1)}) fusion(pred[256,512]{0,1:T(8,128)(4,1)S(1)} %compare_and_fusion, bf16[256,2,8,128]{3,0,2,1:T(8,128)(2,1)S(1)} %get-tuple-element.235, bf16[512,2,128,1]{2,1,0,3:T(2,128)(2,1)S(1)} %bitcast.45), kind=kOutput, calls=%fused_computation.4 | convolution fusion | flops 543158272 | bytes 9846784 | tf_op jit(solution)/shard_map/while/body/eval_jaxpr/cond/branch_1_fun/rkgd,pkd->kgrp/dot_general | solution.py:27
  49.4 2.0 %fusion.4 = f32[2,8,256]{2,1,0:T(8,128)S(1)} fusion(f32[2,512,256,8]{2,1,3,0:T(8,128)S(1)} %get-tuple-element.398, f32[2,8,256]{2,1,0:T(8,128)S(1)} %max.6, pred[256,512]{0,1:T(8,128)(4,1)S(1)} %compare_and_fusion), kind=kLoop, calls=%fused_computation.6 | loop fusion | flops 10481664 | bytes 8552448 | tf_op jit(solution)/shard_map/while/body/eval_jaxpr/cond/branch_1_fun/reduce_sum | solution.py:38
  51.4 0.0 copy-done
  51.4 3.4 %multiply_add_fusion = f32[2,8,256,128]{3,2,1,0:T(8,128)S(1)} fusion(f32[2,8,256,128]{3,2,1,0:T(8,128)S(1)} %copy-done, f32[2,512,256,8]{2,1,3,0:T(8,128)S(1)} %get-tuple-element.398, f32[2,8,256]{2,1,0:T(8,128)S(1)} %max.6, pred[256,512]{0,1:T(8,128)(4,1)S(1)} %compare_and_fusion, f32[2,8,256]{2,1,0:T(8,128)S(1)} %get-tuple-element.396, ...), kind=kOutput, calls=%fused_computation.9 | convolution fusion | flops 548405248 | bytes 13008896 | tf_op jit(solution)/shard_map/while/body/eval_jaxpr/cond/branch_1_fun/kgrp,pkd->kgrd/dot_general | solution.py:39
  54.8 0.0 copy-start.1
  54.9 1.3 %copy-done.1 = f32[2,8,256,128]{3,2,1,0:T(8,128)} copy-done((f32[2,8,256,128]{3,2,1,0:T(8,128)}, f32[2,8,256,128]{3,2,1,0:T(8,128)S(1)}, u32[]{:S(2)}) %copy-start.1) | copy-done | bytes 2097176 | tf_op jit(solution)/shard_map/while/body/eval_jaxpr/cond
  56.2 0.7 dynamic_slice.31
  57.6 0.7 add_compare_fusion.2
  58.3 1.1 %constant_dynamic-slice_fusion.3 = (bf16[1,512,256]{2,1,0:T(8,128)(2,1)S(1)}, bf16[1,512,256]{2,1,0:T(8,128)(2,1)S(1)}) fusion(bf16[2,512,256]{2,1,0:T(8,128)(2,1)} %get-tuple-element.556, s32[]{:T(128)S(6)} %copy.67, bf16[2,512,256]{2,1,0:T(8,128)(2,1)} %get-tuple-element.555), kind=kLoop, calls=%fused_computation.31.clone.1 | loop fusion | bytes 1048580 | tf_op jit(solution)/shard_map/while/body/jit(dynamic_index_in_dim)/dynamic_slice | solution.py:157
  59.4 0.1 squeeze.31
  59.5 0.1 squeeze.32
  59.5 1.1 %broadcast_select_fusion.4 = (bf16[4,128,2,1,128]{4,2,1,0,3:T(2,128)(2,1)S(1)}, bf16[4,128,2,1,128]{4,2,1,0,3:T(2,128)(2,1)S(1)}) fusion(bf16[4,128,2,1,128]{4,2,1,0,3:T(2,128)(2,1)S(1)} %squeeze.31, pred[4,128]{1,0:T(4,128)(4,1)S(1)} %add_compare_fusion.2, bf16[4,128,2,1,128]{4,2,1,0,3:T(2,128)(2,1)S(1)} %squeeze.32), kind=kLoop, calls=%fused_computation.25.clone.1 | loop fusion | flops 262144 | bytes 1049088 | tf_op jit(solution)/shard_map/while/body/eval_jaxpr/jit(_where)/select_n | solution.py:86
  60.6 0.7 pad_maximum_fusion.2
  61.4 0.4 copy.55
  61.8 0.6 gather_fusion
  62.5 0.2 select_select_fusion.2
  62.7 9.3 %conditional.3 = ((f32[2,8,256]{2,1,0:T(8,128)S(1)}, f32[2,8,256]{2,1,0:T(8,128)S(1)}, f32[2,8,256,128]{3,2,1,0:T(8,128)})) conditional(s32[]{:T(128)} %convert_element_type.41, (f32[2,8,256]{2,1,0:T(8,128)S(1)}, f32[2,8,256]{2,1,0:T(8,128)S(1)}, f32[2,8,256,128]{3,2,1,0:T(8,128)}) %tuple.62, (s32[]{:T(128)}, s32[]{:T(128)}, s32[]{:T(128)}, ...), branch_computations={%region_4.4_spmd, %region_5.7_spmd} | conditional | flops 1102325504 | bytes 49553512 | solution.py:137
  62.7 0.7 broadcast_compare_fusion
  63.4 0.2 compare_and_fusion
  63.6 0.1 reshape.144
  63.6 0.1 reshape.145
  63.7 0.0 copy-start
  63.7 1.4 %fusion.2 = (f32[2,8,256]{2,1,0:T(8,128)S(1)}, f32[2,512,256,8]{2,1,3,0:T(8,128)S(1)}) fusion(pred[256,512]{0,1:T(8,128)(4,1)S(1)} %compare_and_fusion, bf16[256,2,8,128]{3,0,2,1:T(8,128)(2,1)S(1)} %get-tuple-element.235, bf16[512,2,128,1]{2,1,0,3:T(2,128)(2,1)S(1)} %bitcast.45), kind=kOutput, calls=%fused_computation.4 | convolution fusion | flops 543158272 | bytes 9846784 | tf_op jit(solution)/shard_map/while/body/eval_jaxpr/cond/branch_1_fun/rkgd,pkd->kgrp/dot_general | solution.py:27
  65.2 2.0 %fusion.4 = f32[2,8,256]{2,1,0:T(8,128)S(1)} fusion(f32[2,512,256,8]{2,1,3,0:T(8,128)S(1)} %get-tuple-element.398, f32[2,8,256]{2,1,0:T(8,128)S(1)} %max.6, pred[256,512]{0,1:T(8,128)(4,1)S(1)} %compare_and_fusion), kind=kLoop, calls=%fused_computation.6 | loop fusion | flops 10481664 | bytes 8552448 | tf_op jit(solution)/shard_map/while/body/eval_jaxpr/cond/branch_1_fun/reduce_sum | solution.py:38
  67.2 0.0 copy-done
  67.2 3.4 %multiply_add_fusion = f32[2,8,256,128]{3,2,1,0:T(8,128)S(1)} fusion(f32[2,8,256,128]{3,2,1,0:T(8,128)S(1)} %copy-done, f32[2,512,256,8]{2,1,3,0:T(8,128)S(1)} %get-tuple-element.398, f32[2,8,256]{2,1,0:T(8,128)S(1)} %max.6, pred[256,512]{0,1:T(8,128)(4,1)S(1)} %compare_and_fusion, f32[2,8,256]{2,1,0:T(8,128)S(1)} %get-tuple-element.396, ...), kind=kOutput, calls=%fused_computation.9 | convolution fusion | flops 548405248 | bytes 13008896 | tf_op jit(solution)/shard_map/while/body/eval_jaxpr/cond/branch_1_fun/kgrp,pkd->kgrd/dot_general | solution.py:39
  70.6 0.0 copy-start.1
  70.6 1.3 %copy-done.1 = f32[2,8,256,128]{3,2,1,0:T(8,128)} copy-done((f32[2,8,256,128]{3,2,1,0:T(8,128)}, f32[2,8,256,128]{3,2,1,0:T(8,128)S(1)}, u32[]{:S(2)}) %copy-start.1) | copy-done | bytes 2097176 | tf_op jit(solution)/shard_map/while/body/eval_jaxpr/cond
  72.0 2.0 %fusion.17 = bf16[256,2,8,128]{3,0,2,1:T(8,128)(2,1)S(1)} fusion(f32[2,8,256,128]{3,2,1,0:T(8,128)} %get-tuple-element.262, f32[2,8,256]{2,1,0:T(8,128)S(1)} %broadcast_select_fusion.2, pred[256]{0:T(512)(128)(4,1)S(1)} %broadcast_compare_fusion.1), kind=kLoop, calls=%fused_computation.35 | loop fusion | flops 1572864 | bytes 3162368 | tf_op jit(solution)/shard_map/convert_element_type | solution.py:53
  74.0 0.7 copy.36
  74.7 1.2 %copy.53 = bf16[32,8,16,128]{3,1,2,0:T(8,128)(2,1)} copy(bf16[32,8,16,128]{3,2,1,0:T(8,128)(2,1)S(1)} %bitcast.47) | data formatting | bytes 2097152
  75.9 1.0 %copy.37 = bf16[4,128,512]{2,1,0:T(8,128)(2,1)} copy(bf16[4,128,512]{1,2,0:T(8,128)(2,1)S(1)} %get-tuple-element.363) | data formatting | bytes 1048576
  (26 shorter events, 0.1 us)
Async XLA Ops:
  47.9 3.5 %copy-start = (f32[2,8,256,128]{3,2,1,0:T(8,128)S(1)}, f32[2,8,256,128]{3,2,1,0:T(8,128)}, u32[]{:S(2)}) copy-start(f32[2,8,256,128]{3,2,1,0:T(8,128)} %get-tuple-element.237) | copy-start | bytes 6291460 | tf_op jit(solution)/shard_map/while/body/eval_jaxpr/cond
  54.8 1.4 %copy-start.1 = (f32[2,8,256,128]{3,2,1,0:T(8,128)}, f32[2,8,256,128]{3,2,1,0:T(8,128)S(1)}, u32[]{:S(2)}) copy-start(f32[2,8,256,128]{3,2,1,0:T(8,128)S(1)} %multiply_add_fusion) | copy-start | bytes 6291460 | tf_op jit(solution)/shard_map/while/body/eval_jaxpr/cond
  63.7 3.5 %copy-start = (f32[2,8,256,128]{3,2,1,0:T(8,128)S(1)}, f32[2,8,256,128]{3,2,1,0:T(8,128)}, u32[]{:S(2)}) copy-start(f32[2,8,256,128]{3,2,1,0:T(8,128)} %get-tuple-element.237) | copy-start | bytes 6291460 | tf_op jit(solution)/shard_map/while/body/eval_jaxpr/cond
  70.6 1.4 %copy-start.1 = (f32[2,8,256,128]{3,2,1,0:T(8,128)}, f32[2,8,256,128]{3,2,1,0:T(8,128)S(1)}, u32[]{:S(2)}) copy-start(f32[2,8,256,128]{3,2,1,0:T(8,128)S(1)} %multiply_add_fusion) | copy-start | bytes 6291460 | tf_op jit(solution)/shard_map/while/body/eval_jaxpr/cond
where the time goes:
time: 77.3 us; the launch traced here: 76.9 us
  blocking collectives  32.7 us (42%)
  local copies, waits for them, and re-layouts  17.1 us (22%)
  other arithmetic  13.6 us (18%)
  matrix products  9.64 us (12%)
  between operations  2.06 us (3%)
  loops' own time  1.84 us (2%)
    all_gather x1, blocking collectives, local(): value_piece = lax.all_gather(values, 'seq', axis=0, tiled=True)  16.4 us
    all_gather x1, blocking collectives, local(): key_piece = lax.all_gather(keys, 'seq', axis=0, tiled=True)  16.3 us
    dot_general x2, matrix products, attend_block(): jnp.einsum('kgrp,pkd->kgrd', weights.astype(jnp.bfloat16), values_split,...  6.81 us
    unnamed x5, local copies, waits for them, and re-layouts  5.16 us
    reduce_sum x2, other arithmetic, attend_block(): denominator = query_state[1] * factor + jnp.sum(weights, axis=-1)  4.01 us
    dynamic_slice x4, local copies, waits for them, and re-layouts, local(): lax.scan(one_block, (states, page_store), (key_blocks, value_blocks, jnp....  3.47 us
    dot_general x2, matrix products, attend_block(): jnp.einsum('rkgd,pkd->kgrp', query_block, keys_split, preferred_element_t...  2.83 us
    cond x10, local copies, waits for them, and re-layouts  2.71 us

commit v1 on v0

--- a/solution.py
+++ b/solution.py
@@ -7,6 +7,17 @@
 HEAD_SIZE = 128
 PAGE_TOKENS = 128
 NEG_FILL = -1e30
+
+
+def pass_along(x, axis, dim):
+    size = lax.axis_size(axis)
+    forward = [(i, (i + 1) % size) for i in range(size)]
+    parts = [x]
+    for far in range(1, size):
+        parts = [lax.ppermute(parts[0], axis, forward), *parts]
+    whole = jnp.concatenate(parts, axis=dim)
+    shift = (lax.axis_index(axis) + 1) * parts[-1].shape[dim]
+    return jnp.roll(whole, shift, axis=dim)
 
 
 def blank_state(kv_heads, group_size, query_count):
@@ -116,7 +127,7 @@
     )
     page_store = jnp.zeros((slots, PAGE_TOKENS, 2 * kv_width), jnp.bfloat16)
     key_piece = lax.all_gather(keys, "seq", axis=0, tiled=True)
-    value_piece = lax.all_gather(values, "seq", axis=0, tiled=True)
+    value_piece = pass_along(values, "seq", 0)
     block_count = key_piece.shape[0] // shard_rows
     per_step = max(1, min(block_count, 512 // shard_rows))
     while block_count % per_step:

time: 77.3 us -> 71.3 us (0.922)
  blocking collectives: 32.7 us -> 16.9 us
  waiting for transfers between devices: 0 us -> 3.76 us
  starting transfers between devices: 0 us -> 3.55 us
  local copies, waits for them, and re-layouts: 17.1 us -> 19.7 us
    all_gather x1 -> x0, blocking collectives: 16.4 us -> none  [local(): value_piece = lax.all_gather(values, 'seq', axis=0, tiled=True)]
    ppermute x0 -> x3, waiting for transfers between devices: none -> 3.76 us  [pass_along(): parts = [lax.ppermute(parts[0], axis, forward), *parts]]
    ppermute x0 -> x3, starting transfers between devices: none -> 3.55 us  [pass_along(): parts = [lax.ppermute(parts[0], axis, forward), *parts]]
    unnamed x5 -> x12, local copies, waits for them, and re-layouts: 5.16 us -> 6.13 us
    concatenate x0 -> x1, local copies, waits for them, and re-layouts: none -> 0.92 us  [pass_along(): return jnp.roll(whole, shift, axis=dim)]
    dynamic_slice x0 -> x1, local copies, waits for them, and re-layouts: none -> 0.84 us  [pass_along(): return jnp.roll(whole, shift, axis=dim)]
  transfers between devices with their start and end apart: 0 -> 3, of which waited for: 0 -> 1; matrix products, arithmetic and copies ran while one was open for 0% -> 6% of each run, Pallas kernels for 0% -> 0%
where the time goes in v1:
time: 71.3 us; the launch traced here: 70.9 us
  local copies, waits for them, and re-layouts  19.7 us (28%)
  blocking collectives  16.9 us (24%)
  other arithmetic  13.6 us (19%)
  matrix products  9.64 us (14%)
  waiting for transfers between devices  3.76 us (5%)
  starting transfers between devices  3.55 us (5%)
  between operations  2.04 us (3%)
  loops' own time  1.81 us (3%)
    all_gather x1, blocking collectives, local(): key_piece = lax.all_gather(keys, 'seq', axis=0, tiled=True)  16.9 us
    dot_general x2, matrix products, attend_block(): jnp.einsum('kgrp,pkd->kgrd', weights.astype(jnp.bfloat16), values_split,...  6.8 us
    unnamed x12, local copies, waits for them, and re-layouts  6.13 us
    reduce_sum x2, other arithmetic, attend_block(): denominator = query_state[1] * factor + jnp.sum(weights, axis=-1)  4.01 us
    ppermute x3, waiting for transfers between devices, pass_along(): parts = [lax.ppermute(parts[0], axis, forward), *parts]  3.76 us
    ppermute x3, starting transfers between devices, pass_along(): parts = [lax.ppermute(parts[0], axis, forward), *parts]  3.55 us
    dynamic_slice x4, local copies, waits for them, and re-layouts, local(): lax.scan(one_block, (states, page_store), (key_blocks, value_blocks, jnp....  3.43 us
    dot_general x2, matrix products, attend_block(): jnp.einsum('rkgd,pkd->kgrp', query_block, keys_split, preferred_element_t...  2.83 us
  transfers between devices with their start and end apart: 3, of which 1 were waited for; matrix products, arithmetic and copies ran while one was open for 6% of the time, Pallas kernels for 0%

profile of v1, /device:TPU:26, one launch (start us, length us, event | category | flops | bytes accessed | tf_op | source)
XLA Modules:
  0.0 70.9 jit_solution(614954022146319595)
XLA Ops:
  0.6 0.3 collective-permute-start
  0.9 0.8 %copy.34 = s32[4,2]{1,0:T(4,128)S(1)} copy(s32[4,2]{0,1:T(2,128)} %param.13) | data formatting | bytes 64 | tf_op args[4]
  1.7 0.1 broadcast_in_dim_reshape.2
  1.8 16.9 %all_gather.3 = bf16[1024,256]{1,0:T(8,128)(2,1)} all-gather(bf16[256,256]{1,0:T(8,128)(2,1)} %param.10), channel_id=1, replica_groups=mesh['groups'=2,'seq'=4,'head'=4] {'seq'}, dimensions={0}, use_global_device_ids=true | all-gather | bytes 655360 | tf_op jit(solution)/shard_map/all_gather | solution.py:129
  18.6 0.2 convert_reduce_fusion
  18.8 0.0 collective-permute-done
  18.8 1.0 %collective-permute-start.1 = (bf16[256,256]{1,0:T(8,128)(2,1)S(1)}, bf16[256,256]{1,0:T(8,128)(2,1)S(1)}, u32[]{:S(2)}, u32[]{:S(2)}) collective-permute-start(bf16[256,256]{1,0:T(8,128)(2,1)S(1)} %collective-permute-done), channel_id=1, source_target_pairs={{0,4},{4,8},{8,12},{12,0},{1,5},{5,9},{9,13},{13,1},{2,6},{6,10},{... | collective-permute-start | bytes 393224 | tf_op jit(solution)/shard_map/ppermute | solution.py:17
  20.5 0.1 fusion.20
  20.6 3.8 %collective-permute-done.1 = bf16[256,256]{1,0:T(8,128)(2,1)S(1)} collective-permute-done((bf16[256,256]{1,0:T(8,128)(2,1)S(1)}, bf16[256,256]{1,0:T(8,128)(2,1)S(1)}, u32[]{:S(2)}, u32[]{:S(2)}) %collective-permute-start.1) | collective-permute-done | bytes 131104 | tf_op jit(solution)/shard_map/ppermute | solution.py:17
  24.4 2.2 %collective-permute-start.2 = (bf16[256,256]{1,0:T(8,128)(2,1)S(1)}, bf16[256,256]{1,0:T(8,128)(2,1)S(1)}, u32[]{:S(2)}, u32[]{:S(2)}) collective-permute-start(bf16[256,256]{1,0:T(8,128)(2,1)S(1)} %collective-permute-done.1), channel_id=1, source_target_pairs={{0,4},{4,8},{8,12},{12,0},{1,5},{5,9},{9,13},{13,1},{2,6},{6,10},{... | collective-permute-start | bytes 393224 | tf_op jit(solution)/shard_map/ppermute | solution.py:17
  26.6 0.6 slice.5
  27.2 1.5 %copy.33 = bf16[256,2048]{0,1:T(8,128)(2,1)S(1)} copy(bf16[256,2048]{1,0:T(8,128)(2,1)} %param.9) | data formatting | bytes 2097152 | tf_op args[0]
  28.7 0.7 copy.35
  30.0 0.1 select_reduce_fusion
  30.1 0.0 collective-permute-done.2
  30.2 0.9 %constant_dynamic-update-slice_fusion.4 = bf16[2048,256]{1,0:T(8,128)(2,1)S(1)} fusion(bf16[2048,256]{1,0:T(8,128)(2,1)S(1)} %constant_dynamic-update-slice_fusion.5, bf16[256,256]{1,0:T(8,128)(2,1)} %param.11), kind=kLoop, calls=%fused_computation.40 | loop fusion | bytes 262144
  31.2 0.9 %constant_dynamic-update-slice_fusion = bf16[2048,256]{1,0:T(8,128)(2,1)S(1)} fusion(bf16[2048,256]{1,0:T(8,128)(2,1)S(1)} %constant_dynamic-update-slice_fusion.1, bf16[256,256]{1,0:T(8,128)(2,1)} %param.11), kind=kLoop, calls=%fused_computation.36 | loop fusion | bytes 262144 | tf_op jit(solution)/shard_map/jit(_roll_dynamic)/concatenate | solution.py:20
  32.1 0.8 %constant_dynamic-slice_fusion.2 = bf16[1024,256]{1,0:T(8,128)(2,1)} fusion(bf16[2048,256]{1,0:T(8,128)(2,1)S(1)} %constant_dynamic-update-slice_fusion, s32[]{:T(128)S(6)} %select_n.92), kind=kLoop, calls=%fused_computation.55 | loop fusion | bytes 1048580 | tf_op jit(solution)/shard_map/jit(_roll_dynamic)/dynamic_slice | solution.py:20
  32.9 1.6 %broadcast_in_dim.106 = f32[2,8,256,128]{3,2,1,0:T(8,128)} broadcast(f32[]{:T(128)} %constant.121.clone.1), dimensions={} | broadcast | bytes 2097156 | tf_op jit(solution)/shard_map/broadcast_in_dim | solution.py:27
  34.5 31.4 %while.20 = (s32[]{:T(128)}, f32[2,8,256]{2,1,0:T(8,128)S(1)}, f32[2,8,256]{2,1,0:T(8,128)S(1)}, f32[2,8,256,128]{3,2,1,0:T(8,128)}, bf16[4,128,512]{1,2,0:T(8,1...) while((s32[]{:T(128)}, f32[2,8,256]{2,1,0:T(8,128)S(1)}, ...), condition=%wide.region_8.9_spmd.clone, body=%wide.region_3.8_spmd.clone.sunk | while | flops 1103377152 | bytes 57424572 | solution.py:168
  34.5 0.6 dynamic_slice.37
  35.9 0.7 add_compare_fusion.2
  36.6 1.1 %constant_dynamic-slice_fusion.4 = (bf16[1,512,256]{2,1,0:T(8,128)(2,1)S(1)}, bf16[1,512,256]{2,1,0:T(8,128)(2,1)S(1)}) fusion(bf16[2,512,256]{2,1,0:T(8,128)(2,1)} %get-tuple-element.556, s32[]{:T(128)S(6)} %copy.74, bf16[2,512,256]{2,1,0:T(8,128)(2,1)} %get-tuple-element.555), kind=kLoop, calls=%fused_computation.31.clone.1 | loop fusion | bytes 1048580 | tf_op jit(solution)/shard_map/while/body/jit(dynamic_index_in_dim)/dynamic_slice | solution.py:168
  37.6 0.1 squeeze.31
  37.7 0.1 squeeze.32
  37.8 1.1 %broadcast_select_fusion.4 = (bf16[4,128,2,1,128]{4,2,1,0,3:T(2,128)(2,1)S(1)}, bf16[4,128,2,1,128]{4,2,1,0,3:T(2,128)(2,1)S(1)}) fusion(bf16[4,128,2,1,128]{4,2,1,0,3:T(2,128)(2,1)S(1)} %squeeze.31, pred[4,128]{1,0:T(4,128)(4,1)S(1)} %add_compare_fusion.2, bf16[4,128,2,1,128]{4,2,1,0,3:T(2,128)(2,1)S(1)} %squeeze.32), kind=kLoop, calls=%fused_computation.25.clone.1 | loop fusion | flops 262144 | bytes 1049088 | tf_op jit(solution)/shard_map/while/body/eval_jaxpr/jit(_where)/select_n | solution.py:97
  38.9 0.7 %pad_maximum_fusion.2 = bf16[4,128,2,2,128]{4,2,1,0,3:T(2,128)(2,1)S(1)} fusion(bf16[4,128,2,1,128]{4,2,1,0,3:T(2,128)(2,1)S(1)} %get-tuple-element.500, bf16[4,128,2,1,128]{4,2,1,0,3:T(2,128)(2,1)S(1)} %get-tuple-element.501), kind=kLoop, calls=%fused_computation.22.clone.1 | loop fusion | flops 262144 | bytes 1048576 | tf_op jit(solution)/shard_map/while/body/eval_jaxpr/stack | solution.py:70
  39.7 0.4 copy.55
  40.1 0.6 gather_fusion
  40.8 0.2 select_select_fusion.2
  40.9 9.3 %conditional.3 = ((f32[2,8,256]{2,1,0:T(8,128)S(1)}, f32[2,8,256]{2,1,0:T(8,128)S(1)}, f32[2,8,256,128]{3,2,1,0:T(8,128)})) conditional(s32[]{:T(128)} %convert_element_type.41, (f32[2,8,256]{2,1,0:T(8,128)S(1)}, f32[2,8,256]{2,1,0:T(8,128)S(1)}, f32[2,8,256,128]{3,2,1,0:T(8,128)}) %tuple.62, (s32[]{:T(128)}, s32[]{:T(128)}, s32[]{:T(128)}, ...), branch_computations={%region_4.4_spmd, %region_5.7_spmd} | conditional | flops 1102325504 | bytes 49553512 | solution.py:148
  40.9 0.7 broadcast_compare_fusion
  41.6 0.2 compare_and_fusion
  41.8 0.1 reshape.144
  41.9 0.1 reshape.145
  42.0 0.0 copy-start
  42.0 1.4 %fusion.2 = (f32[2,8,256]{2,1,0:T(8,128)S(1)}, f32[2,512,256,8]{2,1,3,0:T(8,128)S(1)}) fusion(pred[256,512]{0,1:T(8,128)(4,1)S(1)} %compare_and_fusion, bf16[256,2,8,128]{3,0,2,1:T(8,128)(2,1)S(1)} %get-tuple-element.235, bf16[512,2,128,1]{2,1,0,3:T(2,128)(2,1)S(1)} %bitcast.45), kind=kOutput, calls=%fused_computation.4 | convolution fusion | flops 543158272 | bytes 9846784 | tf_op jit(solution)/shard_map/while/body/eval_jaxpr/cond/branch_1_fun/rkgd,pkd->kgrp/dot_general | solution.py:38
  43.4 2.0 %fusion.4 = f32[2,8,256]{2,1,0:T(8,128)S(1)} fusion(f32[2,512,256,8]{2,1,3,0:T(8,128)S(1)} %get-tuple-element.398, f32[2,8,256]{2,1,0:T(8,128)S(1)} %max.6, pred[256,512]{0,1:T(8,128)(4,1)S(1)} %compare_and_fusion), kind=kLoop, calls=%fused_computation.6 | loop fusion | flops 10481664 | bytes 8552448 | tf_op jit(solution)/shard_map/while/body/eval_jaxpr/cond/branch_1_fun/reduce_sum | solution.py:49
  45.5 3.4 %multiply_add_fusion = f32[2,8,256,128]{3,2,1,0:T(8,128)S(1)} fusion(f32[2,8,256,128]{3,2,1,0:T(8,128)S(1)} %copy-done, f32[2,512,256,8]{2,1,3,0:T(8,128)S(1)} %get-tuple-element.398, f32[2,8,256]{2,1,0:T(8,128)S(1)} %max.6, pred[256,512]{0,1:T(8,128)(4,1)S(1)} %compare_and_fusion, f32[2,8,256]{2,1,0:T(8,128)S(1)} %get-tuple-element.396, ...), kind=kOutput, calls=%fused_computation.9 | convolution fusion | flops 548405248 | bytes 13008896 | tf_op jit(solution)/shard_map/while/body/eval_jaxpr/cond/branch_1_fun/kgrp,pkd->kgrd/dot_general | solution.py:50
  48.9 1.3 %copy-done.1 = f32[2,8,256,128]{3,2,1,0:T(8,128)} copy-done((f32[2,8,256,128]{3,2,1,0:T(8,128)}, f32[2,8,256,128]{3,2,1,0:T(8,128)S(1)}, u32[]{:S(2)}) %copy-start.1) | copy-done | bytes 2097176 | tf_op jit(solution)/shard_map/while/body/eval_jaxpr/cond
  50.2 0.6 dynamic_slice.37
  51.6 0.7 add_compare_fusion.2
  52.3 1.1 %constant_dynamic-slice_fusion.4 = (bf16[1,512,256]{2,1,0:T(8,128)(2,1)S(1)}, bf16[1,512,256]{2,1,0:T(8,128)(2,1)S(1)}) fusion(bf16[2,512,256]{2,1,0:T(8,128)(2,1)} %get-tuple-element.556, s32[]{:T(128)S(6)} %copy.74, bf16[2,512,256]{2,1,0:T(8,128)(2,1)} %get-tuple-element.555), kind=kLoop, calls=%fused_computation.31.clone.1 | loop fusion | bytes 1048580 | tf_op jit(solution)/shard_map/while/body/jit(dynamic_index_in_dim)/dynamic_slice | solution.py:168
  53.4 0.1 squeeze.31
  53.4 0.1 squeeze.32
  53.5 1.1 %broadcast_select_fusion.4 = (bf16[4,128,2,1,128]{4,2,1,0,3:T(2,128)(2,1)S(1)}, bf16[4,128,2,1,128]{4,2,1,0,3:T(2,128)(2,1)S(1)}) fusion(bf16[4,128,2,1,128]{4,2,1,0,3:T(2,128)(2,1)S(1)} %squeeze.31, pred[4,128]{1,0:T(4,128)(4,1)S(1)} %add_compare_fusion.2, bf16[4,128,2,1,128]{4,2,1,0,3:T(2,128)(2,1)S(1)} %squeeze.32), kind=kLoop, calls=%fused_computation.25.clone.1 | loop fusion | flops 262144 | bytes 1049088 | tf_op jit(solution)/shard_map/while/body/eval_jaxpr/jit(_where)/select_n | solution.py:97
  54.6 0.7 %pad_maximum_fusion.2 = bf16[4,128,2,2,128]{4,2,1,0,3:T(2,128)(2,1)S(1)} fusion(bf16[4,128,2,1,128]{4,2,1,0,3:T(2,128)(2,1)S(1)} %get-tuple-element.500, bf16[4,128,2,1,128]{4,2,1,0,3:T(2,128)(2,1)S(1)} %get-tuple-element.501), kind=kLoop, calls=%fused_computation.22.clone.1 | loop fusion | flops 262144 | bytes 1048576 | tf_op jit(solution)/shard_map/while/body/eval_jaxpr/stack | solution.py:70
  55.4 0.4 copy.55
  55.8 0.6 gather_fusion
  56.5 0.2 select_select_fusion.2
  56.6 9.3 %conditional.3 = ((f32[2,8,256]{2,1,0:T(8,128)S(1)}, f32[2,8,256]{2,1,0:T(8,128)S(1)}, f32[2,8,256,128]{3,2,1,0:T(8,128)})) conditional(s32[]{:T(128)} %convert_element_type.41, (f32[2,8,256]{2,1,0:T(8,128)S(1)}, f32[2,8,256]{2,1,0:T(8,128)S(1)}, f32[2,8,256,128]{3,2,1,0:T(8,128)}) %tuple.62, (s32[]{:T(128)}, s32[]{:T(128)}, s32[]{:T(128)}, ...), branch_computations={%region_4.4_spmd, %region_5.7_spmd} | conditional | flops 1102325504 | bytes 49553512 | solution.py:148
  56.7 0.7 broadcast_compare_fusion
  57.3 0.2 compare_and_fusion
  57.5 0.1 reshape.144
  57.6 0.1 reshape.145
  57.7 0.0 copy-start
  57.7 1.4 %fusion.2 = (f32[2,8,256]{2,1,0:T(8,128)S(1)}, f32[2,512,256,8]{2,1,3,0:T(8,128)S(1)}) fusion(pred[256,512]{0,1:T(8,128)(4,1)S(1)} %compare_and_fusion, bf16[256,2,8,128]{3,0,2,1:T(8,128)(2,1)S(1)} %get-tuple-element.235, bf16[512,2,128,1]{2,1,0,3:T(2,128)(2,1)S(1)} %bitcast.45), kind=kOutput, calls=%fused_computation.4 | convolution fusion | flops 543158272 | bytes 9846784 | tf_op jit(solution)/shard_map/while/body/eval_jaxpr/cond/branch_1_fun/rkgd,pkd->kgrp/dot_general | solution.py:38
  59.1 2.0 %fusion.4 = f32[2,8,256]{2,1,0:T(8,128)S(1)} fusion(f32[2,512,256,8]{2,1,3,0:T(8,128)S(1)} %get-tuple-element.398, f32[2,8,256]{2,1,0:T(8,128)S(1)} %max.6, pred[256,512]{0,1:T(8,128)(4,1)S(1)} %compare_and_fusion), kind=kLoop, calls=%fused_computation.6 | loop fusion | flops 10481664 | bytes 8552448 | tf_op jit(solution)/shard_map/while/body/eval_jaxpr/cond/branch_1_fun/reduce_sum | solution.py:49
  61.2 3.4 %multiply_add_fusion = f32[2,8,256,128]{3,2,1,0:T(8,128)S(1)} fusion(f32[2,8,256,128]{3,2,1,0:T(8,128)S(1)} %copy-done, f32[2,512,256,8]{2,1,3,0:T(8,128)S(1)} %get-tuple-element.398, f32[2,8,256]{2,1,0:T(8,128)S(1)} %max.6, pred[256,512]{0,1:T(8,128)(4,1)S(1)} %compare_and_fusion, f32[2,8,256]{2,1,0:T(8,128)S(1)} %get-tuple-element.396, ...), kind=kOutput, calls=%fused_computation.9 | convolution fusion | flops 548405248 | bytes 13008896 | tf_op jit(solution)/shard_map/while/body/eval_jaxpr/cond/branch_1_fun/kgrp,pkd->kgrd/dot_general | solution.py:50
  64.6 1.3 %copy-done.1 = f32[2,8,256,128]{3,2,1,0:T(8,128)} copy-done((f32[2,8,256,128]{3,2,1,0:T(8,128)}, f32[2,8,256,128]{3,2,1,0:T(8,128)S(1)}, u32[]{:S(2)}) %copy-start.1) | copy-done | bytes 2097176 | tf_op jit(solution)/shard_map/while/body/eval_jaxpr/cond
  66.0 2.0 %fusion.17 = bf16[256,2,8,128]{3,0,2,1:T(8,128)(2,1)S(1)} fusion(f32[2,8,256,128]{3,2,1,0:T(8,128)} %get-tuple-element.262, f32[2,8,256]{2,1,0:T(8,128)S(1)} %broadcast_select_fusion.2, pred[256]{0:T(512)(128)(4,1)S(1)} %broadcast_compare_fusion.1), kind=kLoop, calls=%fused_computation.35 | loop fusion | flops 1572864 | bytes 3162368 | tf_op jit(solution)/shard_map/convert_element_type | solution.py:64
  68.0 0.7 copy.36
  68.7 1.2 %copy.53 = bf16[32,8,16,128]{3,1,2,0:T(8,128)(2,1)} copy(bf16[32,8,16,128]{3,2,1,0:T(8,128)(2,1)S(1)} %bitcast.47) | data formatting | bytes 2097152
  69.9 1.0 %copy.37 = bf16[4,128,512]{2,1,0:T(8,128)(2,1)} copy(bf16[4,128,512]{1,2,0:T(8,128)(2,1)S(1)} %get-tuple-element.363) | data formatting | bytes 1048576
  (36 shorter events, 0.2 us)
Async XLA Ops:
  0.6 18.2 %collective-permute-start = (bf16[256,256]{1,0:T(8,128)(2,1)}, bf16[256,256]{1,0:T(8,128)(2,1)S(1)}, u32[]{:S(2)}, u32[]{:S(2)}) collective-permute-start(bf16[256,256]{1,0:T(8,128)(2,1)} %param.11), channel_id=1, source_target_pairs={{0,4},{4,8},{8,12},{12,0},{1,5},{5,9},{9,13},{13,1},{2,6},{6,10},{... | collective-permute-start | bytes 393224 | tf_op jit(solution)/shard_map/ppermute | solution.py:17
  18.8 5.6 %collective-permute-start.1 = (bf16[256,256]{1,0:T(8,128)(2,1)S(1)}, bf16[256,256]{1,0:T(8,128)(2,1)S(1)}, u32[]{:S(2)}, u32[]{:S(2)}) collective-permute-start(bf16[256,256]{1,0:T(8,128)(2,1)S(1)} %collective-permute-done), channel_id=1, source_target_pairs={{0,4},{4,8},{8,12},{12,0},{1,5},{5,9},{9,13},{13,1},{2,6},{6,10},{... | collective-permute-start | bytes 393224 | tf_op jit(solution)/shard_map/ppermute | solution.py:17
  24.4 5.8 %collective-permute-start.2 = (bf16[256,256]{1,0:T(8,128)(2,1)S(1)}, bf16[256,256]{1,0:T(8,128)(2,1)S(1)}, u32[]{:S(2)}, u32[]{:S(2)}) collective-permute-start(bf16[256,256]{1,0:T(8,128)(2,1)S(1)} %collective-permute-done.1), channel_id=1, source_target_pairs={{0,4},{4,8},{8,12},{12,0},{1,5},{5,9},{9,13},{13,1},{2,6},{6,10},{... | collective-permute-start | bytes 393224 | tf_op jit(solution)/shard_map/ppermute | solution.py:17
  42.0 3.5 %copy-start = (f32[2,8,256,128]{3,2,1,0:T(8,128)S(1)}, f32[2,8,256,128]{3,2,1,0:T(8,128)}, u32[]{:S(2)}) copy-start(f32[2,8,256,128]{3,2,1,0:T(8,128)} %get-tuple-element.237) | copy-start | bytes 6291460 | tf_op jit(solution)/shard_map/while/body/eval_jaxpr/cond
  48.9 1.4 %copy-start.1 = (f32[2,8,256,128]{3,2,1,0:T(8,128)}, f32[2,8,256,128]{3,2,1,0:T(8,128)S(1)}, u32[]{:S(2)}) copy-start(f32[2,8,256,128]{3,2,1,0:T(8,128)S(1)} %multiply_add_fusion) | copy-start | bytes 6291460 | tf_op jit(solution)/shard_map/while/body/eval_jaxpr/cond
  57.7 3.5 %copy-start = (f32[2,8,256,128]{3,2,1,0:T(8,128)S(1)}, f32[2,8,256,128]{3,2,1,0:T(8,128)}, u32[]{:S(2)}) copy-start(f32[2,8,256,128]{3,2,1,0:T(8,128)} %get-tuple-element.237) | copy-start | bytes 6291460 | tf_op jit(solution)/shard_map/while/body/eval_jaxpr/cond
  64.6 1.4 %copy-start.1 = (f32[2,8,256,128]{3,2,1,0:T(8,128)}, f32[2,8,256,128]{3,2,1,0:T(8,128)S(1)}, u32[]{:S(2)}) copy-start(f32[2,8,256,128]{3,2,1,0:T(8,128)S(1)} %multiply_add_fusion) | copy-start | bytes 6291460 | tf_op jit(solution)/shard_map/while/body/eval_jaxpr/cond
